TPU v7x, 256 devices: a whole 4x4x8 slice. The times are simulated.
256 devices in a mesh: vocab: 32 (over z, y), section: 8 (over x, core).
Axes of the slice: x: 4, y: 4, z: 8, core: 2. Of those that a mesh axis runs over, the one named last changes fastest.
Arguments:
- hidden: bfloat16 [512, 8192], P('section', 'vocab'), may hold values from -2 to 2
- targets: int32 [512], replicated, may hold values from 0 to 98303
- out_weight: bfloat16 [98304, 8192], P(('vocab', 'section')), may hold values from -2 to 2
Outputs:
- token_loss: float32 [512], replicated
- weight_grad: bfloat16 [98304, 8192], P(('vocab', 'section'))
- sent_grad: bfloat16 [512, 8192], P('section', 'vocab')
All inputs are finite; a program needn't handle non-finite values.
Results may differ from a plain program's by a relative error of at most 0.0033.
Values may be sent and summed in bfloat16 or wider, within the bound.
A program may use at most 128 MiB of HBM per device.

v0:
```python
import jax
import jax.numpy as jnp
from jax import lax
from jax.sharding import Mesh
from jax.sharding import PartitionSpec as P

VOCAB = ("vocab_0", "vocab_1")
SECTION = ("section_0", "section_1")
VOCAB_SECTION = ("vocab_0", "vocab_1", "section_0", "section_1")


def sent_to_all(value, axis):
    copies = jnp.broadcast_to(value, (lax.axis_size(axis), *value.shape))
    return lax.all_to_all(copies, axis, split_axis=0, concat_axis=0, tiled=True)


def laid_out(blocks, dim):
    blocks = jnp.moveaxis(blocks, 0, dim)
    dims = blocks.shape
    return blocks.reshape(*dims[:dim], dims[dim] * dims[dim + 1], *dims[dim + 2 :])


def gathered_copies(value, axis, dim):
    blocks = sent_to_all(value, axis)
    return laid_out(blocks, dim)


def collected_together(value, axis):
    leaves = jax.tree.leaves(value)
    sequence = sorted(range(len(leaves)), key=lambda k: -leaves[k].size)
    width = (1, *leaves[sequence[0]].shape)[-1]
    lines = [
        jnp.pad(leaves[k].reshape(-1), (0, -leaves[k].size % width)).reshape(-1, width)
        for k in sequence
    ]
    both, at, found = (lax.all_gather(jnp.concatenate(lines), axis), 0, {})
    for k, line in zip(sequence, lines):
        piece = both[:, at : at + len(line)].reshape(len(both), -1)
        found[k] = piece[:, : leaves[k].size].reshape(-1, *leaves[k].shape)
        at += len(line)
    numbers = iter(range(len(leaves)))
    return jax.tree.map(lambda _: found[next(numbers)], value)


def combined_by_axis(value, axes, combine):
    for axis in axes:
        pieces = collected_together(value, axis)
        value = jax.tree.map(lambda part: part[0], pieces)
        for k in range(1, lax.axis_size(axis)):
            value = combine(value, jax.tree.map(lambda part: part[k], pieces))
    return value


def split_up(value, dim, devices):
    before, after = (value.shape[:dim], value.shape[dim + 1 :])
    return jnp.moveaxis(value.reshape(*before, devices, -1, *after), dim, 0)


def summed_on_arrival(value, axis, dim):
    blocks = split_up(value, dim, lax.axis_size(axis))
    arrived = lax.all_to_all(blocks, axis, split_axis=0, concat_axis=0, tiled=True)
    return arrived.sum(axis=0)


def shifted(value, axis, steps):
    count = lax.axis_size(axis)
    pairs = [(source, (source + steps) % count) for source in range(count)]
    return lax.ppermute(value, axis, pairs)


def combine(first, second):
    top_a, sum_a, hit_a = first
    top_b, sum_b, hit_b = second
    top = jnp.maximum(top_a, top_b)
    return (top, sum_a * jnp.exp(top_a - top) + sum_b * jnp.exp(top_b - top), hit_a + hit_b)


def on_device(hidden, targets, out_weight):
    columns = gathered_copies(hidden, VOCAB, 1)
    whole = lax.all_gather(columns, SECTION, axis=0, tiled=True)
    rows = out_weight.shape[0]
    offset = lax.axis_index(VOCAB_SECTION) * rows
    logits = jnp.einsum("td,vd->tv", whole, out_weight, preferred_element_type=jnp.float32)
    picked = targets[:, None] - offset == jnp.arange(rows, dtype=jnp.int32)[None, :]
    local_hit = jnp.sum(jnp.where(picked, logits, jnp.float32(0.0)), axis=1)
    local_top = jnp.max(logits, axis=1)
    local_sum = jnp.sum(jnp.exp(logits - local_top[:, None]), axis=1)
    top, total, target_logit = combined_by_axis(
        (local_top, local_sum, local_hit), VOCAB_SECTION, combine
    )
    token_loss = top + jnp.log(total) - target_logit
    probs = jnp.exp(logits - top[:, None]) / total[:, None]
    dlogits = (probs - picked.astype(jnp.float32)).astype(jnp.bfloat16)
    weight_grad = jnp.einsum(
        "tv,td->vd", dlogits, whole, preferred_element_type=jnp.float32
    ).astype(jnp.bfloat16)
    token_block = lax.psum_scatter(
        jnp.dot(dlogits, out_weight, preferred_element_type=jnp.float32),
        SECTION,
        scatter_dimension=0,
        tiled=True,
    )
    owned = summed_on_arrival(token_block, VOCAB, 1)
    sent_grad = shifted(owned.astype(jnp.bfloat16), SECTION, -1)
    return (token_loss, weight_grad, sent_grad)


def solution(mesh):
    split = Mesh(mesh.devices.reshape(8, 4, 4, 2), ("vocab_0", "vocab_1", "section_0", "section_1"))
    placed = (P(SECTION, VOCAB), P(), P(VOCAB_SECTION, None))
    return jax.shard_map(
        on_device,
        mesh=split,
        in_specs=placed,
        out_specs=(P(), P(VOCAB_SECTION, None), P(SECTION, VOCAB)),
        check_vma=False,
    )
```

profile of v0, /device:TPU:1, one launch (start us, length us, event | category | flops | bytes accessed | tf_op | source)
XLA Modules:
  0.0 341.3 jit_solution(13021333229469894591)
XLA Ops:
  7.2 0.0 copy-start
  7.2 0.0 all-gather.10.cloned.1.call-start
  7.2 0.9 broadcast_in_dim.6
  8.1 38.0 %all_to_all.10 = bf16[32,64,256]{2,1,0:T(8,128)(2,1)S(1)} all-to-all(bf16[32,64,256]{2,1,0:T(8,128)(2,1)S(1)} %broadcast_in_dim.6), channel_id=1, replica_groups=mesh['vocab_0'=8,'vocab_1'=4,'section_0'=4,'section_1'=2] {'vocab_0','vo..., dimensions={0} | all-to-all | bytes 2097152 | tf_op jit(solution)/shard_map/all_to_all | solution.py:14
  46.1 1.0 copy.9
  47.2 0.0 all-gather.10.cloned.1.call-update
  47.2 0.0 reduce-scatter.2.cloned.1.call-start
  47.2 0.0 copy-done
  47.3 51.9 %all-gather.10.cloned.1.call-done = bf16[512,8192]{1,0:T(8,128)(2,1)} async-done(((bf16[64,8192]{1,0:T(8,128)(2,1)}), bf16[512,8192]{1,0:T(8,128)(2,1)}) %all-gather.10.cloned.1.call-update) | async-done | bytes 8388624 | tf_op jit(solution)/shard_map/all_gather | solution.py:80
  99.1 7.8 %fusion.60 = (f32[512]{0:T(512)S(1)}, f32[512,384]{0,1:T(8,128)S(1)}) fusion(bf16[512,8192]{1,0:T(8,128)(2,1)} %all-gather.10.cloned.1.call-done, bf16[384,8192]{1,0:T(8,128)(2,1)} %param.5), kind=kOutput, calls=%fused_computation.116 | convolution fusion | flops 3221421568 | bytes 15468544 | tf_op jit(solution)/shard_map/td,vd->tv/dot_general | solution.py:83
  107.0 0.2 exponential_reduce_fusion
  107.2 19.7 %all-gather.4 = f32[8,3,512]{2,1,0:T(4,128)S(1)} all-gather(f32[1,3,512]{2,1,0:T(4,128)S(1)} %maximum_bitcast_fusion), channel_id=2, replica_groups=mesh['vocab_0'=8,'vocab_1'=4,'section_0'=4,'section_1'=2] {'vocab_0'}, dimensions={0}, use_global_device_ids=true | all-gather | bytes 55296 | tf_op jit(solution)/shard_map/all_gather | solution.py:36
  126.9 0.1 fusion.22
  127.0 9.6 %all-gather.5 = f32[4,3,512]{2,1,0:T(4,128)S(1)} all-gather(f32[1,3,512]{2,1,0:T(4,128)S(1)} %maximum_bitcast_fusion.1), channel_id=3, replica_groups=mesh['vocab_0'=8,'vocab_1'=4,'section_0'=4,'section_1'=2] {'vocab_1'}, dimensions={0}, use_global_device_ids=true | all-gather | bytes 30720 | tf_op jit(solution)/shard_map/all_gather | solution.py:36
  136.7 9.0 %all-gather.6 = f32[4,3,512]{2,1,0:T(4,128)S(1)} all-gather(f32[1,3,512]{2,1,0:T(4,128)S(1)} %maximum_bitcast_fusion.2), channel_id=4, replica_groups=mesh['vocab_0'=8,'vocab_1'=4,'section_0'=4,'section_1'=2] {'section_0'}, dimensions={0}, use_global_device_ids=true | all-gather | bytes 30720 | tf_op jit(solution)/shard_map/all_gather | solution.py:36
  145.8 13.6 %all-gather.7 = f32[2,3,512]{2,1,0:T(4,128)S(1)} all-gather(f32[1,3,512]{2,1,0:T(4,128)S(1)} %maximum_bitcast_fusion.3), channel_id=5, replica_groups=mesh['vocab_0'=8,'vocab_1'=4,'section_0'=4,'section_1'=2] {'section_1'}, dimensions={0}, use_global_device_ids=true | all-gather | bytes 18432 | tf_op jit(solution)/shard_map/all_gather | solution.py:36
  159.4 0.6 add_subtract_fusion
  160.0 10.9 %fusion.55 = f32[512,8192]{1,0:T(8,128)} fusion(bf16[384,8192]{1,0:T(8,128)(2,1)} %param.5, f32[512,384]{0,1:T(8,128)S(1)} %get-tuple-element.20, f32[512]{0:T(512)S(1)} %get-tuple-element.6, f32[512]{0:T(512)S(1)} %get-tuple-element.7, s32[512]{0:T(512)S(1)} %broadcast_subtract_fusion), kind=kOutput, calls=%fused_computation.114 | convolution fusion | flops 3222405120 | bytes 23861248 | tf_op jit(solution)/shard_map/dot_general | solution.py:98
  170.9 0.0 reduce-scatter.2.cloned.1.call-update
  171.0 91.3 %reduce-scatter.2.cloned.1.call-done = f32[64,8192]{1,0:T(8,128)} async-done(((f32[512,8192]{1,0:T(8,128)}), f32[64,8192]{1,0:T(8,128)}) %reduce-scatter.2.cloned.1.call-update) | async-done | bytes 2097168 | tf_op jit(solution)/shard_map/reduce_scatter | solution.py:97
  262.3 1.8 copy.11
  264.1 57.7 %all_to_all.11 = f32[32,64,256]{2,1,0:T(8,128)S(1)} all-to-all(f32[32,64,256]{2,1,0:T(8,128)S(1)} %bitcast.336), channel_id=1, replica_groups=mesh['vocab_0'=8,'vocab_1'=4,'section_0'=4,'section_1'=2] {'vocab_0','vo..., dimensions={0} | all-to-all | bytes 4194304 | tf_op jit(solution)/shard_map/all_to_all | solution.py:61
  321.8 0.1 reduce_sum.29
  322.0 3.1 collective-permute-start
  325.1 8.7 %convolution_convert_fusion = bf16[384,8192]{1,0:T(8,128)(2,1)} fusion(bf16[512,8192]{1,0:T(8,128)(2,1)} %all-gather.10.cloned.1.call-done, f32[512,384]{0,1:T(8,128)S(1)} %get-tuple-element.20, f32[512]{0:T(512)S(1)} %get-tuple-element.6, f32[512]{0:T(512)S(1)} %get-tuple-element.7, s32[512]{0:T(512)S(1)} %broadcast_subtract_fusion), kind=kOutput, calls=%fused_computation | convolution fusion | flops 3225550848 | bytes 15472640 | tf_op jit(solution)/shard_map/tv,td->vd/dot_general | solution.py:94
  333.8 0.0 collective-permute-done
  333.8 0.6 copy.13
  (11 shorter events, 0.2 us)
Async XLA Ops:
  7.2 40.1 %copy-start = (s32[512]{0:T(512)S(1)}, s32[512]{0:T(512)}, u32[]{:S(2)}) copy-start(s32[512]{0:T(512)} %param.4) | copy-start | bytes 6148
  7.2 91.9 %all-gather.10.cloned.1.call-start = ((), (), s32[]{:S(2)}) async-start(), calls=%async_computation.3 | async-start | bytes 9437184 | tf_op jit(solution)/shard_map/all_gather | solution.py:80
  47.2 215.1 %reduce-scatter.2.cloned.1.call-start = ((), (), s32[]{:S(2)}) async-start(), calls=%async_computation.4 | async-start | bytes 18874368 | tf_op jit(solution)/shard_map/reduce_scatter | solution.py:97
  322.0 11.9 %collective-permute-start = (bf16[64,256]{1,0:T(8,128)(2,1)S(1)}, bf16[64,256]{1,0:T(8,128)(2,1)S(1)}, u32[]{:S(2)}, u32[]{:S(2)}) collective-permute-start(bf16[64,256]{1,0:T(8,128)(2,1)S(1)} %reduce_sum.29), channel_id=1, source_target_pairs={{0,7},{1,0},{2,1},{3,2},{4,3},{5,4},{6,5},{7,6},{8,15},{9,8},{10,9... | collective-permute-start | bytes 98312 | tf_op jit(solution)/shard_map/ppermute | solution.py:68
Sparse Core Ops, SparseCore 0:
  47.3 51.7 all-gather.9
  171.1 91.1 reduce-scatter.1
where the time goes:
time: 342 us; the launch traced here: 341 us
  blocking collectives  148 us (43%)
  waiting for transfers between devices  143 us (42%)
  matrix products  27.5 us (8%)
  between operations  14.2 us (4%)
  local copies, waits for them, and re-layouts  4.34 us (1%)
    reduce_scatter x1, waiting for transfers between devices, on_device(): lax.psum_scatter(jnp.dot(dlogits, out_weight, preferred_element_type=jnp....  91.3 us
    all_to_all x1, blocking collectives, summed_on_arrival(): lax.all_to_all(blocks, axis, split_axis=0, concat_axis=0, tiled=True)  57.7 us
    all_gather x4, blocking collectives, collected_together(): both, at, found = (lax.all_gather(jnp.concatenate(lines), axis), 0, {})  52 us
    all_gather x1, waiting for transfers between devices, on_device(): whole = lax.all_gather(columns, SECTION, axis=0, tiled=True)  51.9 us
    all_to_all x1, blocking collectives, sent_to_all(): return lax.all_to_all(copies, axis, split_axis=0, concat_axis=0, tiled=True)  38 us
    dot_general x1, matrix products, on_device(): jnp.dot(dlogits, out_weight, preferred_element_type=jnp.float32)  10.9 us
    dot_general x1, matrix products, on_device(): jnp.einsum('tv,td->vd', dlogits, whole, preferred_element_type=jnp.float32)  8.73 us
    dot_general x1, matrix products, on_device(): jnp.einsum('td,vd->tv', whole, out_weight, preferred_element_type=jnp.flo...  7.84 us
  transfers between devices with their start and end apart: 3, of which 2 were waited for; matrix products, arithmetic and copies ran while one was open for 3% of the time, Pallas kernels for 0%

commit v1 on v0

--- a/solution.py
+++ b/solution.py
@@ -77,7 +77,10 @@
 
 def on_device(hidden, targets, out_weight):
     columns = gathered_copies(hidden, VOCAB, 1)
-    whole = lax.all_gather(columns, SECTION, axis=0, tiled=True)
+    whole = jnp.concatenate(
+        lax.all_to_all(jnp.stack([columns for _ in range(lax.psum(1, SECTION))]), SECTION, 0, 0),
+        axis=0,
+    )
     rows = out_weight.shape[0]
     offset = lax.axis_index(VOCAB_SECTION) * rows
     logits = jnp.einsum("td,vd->tv", whole, out_weight, preferred_element_type=jnp.float32)

time: 342 us -> 390 us (1.14)
  waiting for transfers between devices: 143 us -> 183 us
  starting transfers between devices: 3.2 us -> 10.9 us
    all_to_all x0 -> x1, waiting for transfers between devices: none -> 93.7 us  [on_device(): lax.all_to_all(jnp.stack([columns for _ in range(lax.psum(1, SECTION))]),...]
    all_gather x1 -> x0, waiting for transfers between devices: 51.9 us -> none  [on_device(): whole = lax.all_gather(columns, SECTION, axis=0, tiled=True)]
    all_to_all x0 -> x1, starting transfers between devices: none -> 7.76 us  [on_device(): lax.all_to_all(jnp.stack([columns for _ in range(lax.psum(1, SECTION))]),...]
    another operation x0 -> x2, local copies, waits for them, and re-layouts: none -> 4.3 us  [on_device(): jnp.stack([columns for _ in range(lax.psum(1, SECTION))])]
  transfers between devices with their start and end apart: 3 -> 3, of which waited for: 2 -> 2; matrix products, arithmetic and copies ran while one was open for 3% -> 2% of each run, Pallas kernels for 0% -> 0%
where the time goes in v1:
time: 390 us
  waiting for transfers between devices  183 us (47%)
  blocking collectives  147 us (38%)
  matrix products  25.6 us (7%)
  between operations  14.1 us (4%)
  starting transfers between devices  10.9 us (3%)
  local copies, waits for them, and re-layouts  7.61 us (2%)
    all_to_all x1, waiting for transfers between devices, on_device(): lax.all_to_all(jnp.stack([columns for _ in range(lax.psum(1, SECTION))]),...  93.7 us
    reduce_scatter x1, waiting for transfers between devices, on_device(): lax.psum_scatter(jnp.dot(dlogits, out_weight, preferred_element_type=jnp....  89.2 us
    all_to_all x1, blocking collectives, summed_on_arrival(): lax.all_to_all(blocks, axis, split_axis=0, concat_axis=0, tiled=True)  57.7 us
    all_gather x4, blocking collectives, collected_together(): both, at, found = (lax.all_gather(jnp.concatenate(lines), axis), 0, {})  51.5 us
    all_to_all x1, blocking collectives, sent_to_all(): return lax.all_to_all(copies, axis, split_axis=0, concat_axis=0, tiled=True)  38 us
    dot_general x1, matrix products, on_device(): jnp.einsum('td,vd->tv', whole, out_weight, preferred_element_type=jnp.flo...  8.75 us
    dot_general x1, matrix products, on_device(): jnp.einsum('tv,td->vd', dlogits, whole, preferred_element_type=jnp.float32)  8.71 us
    dot_general x1, matrix products, on_device(): jnp.dot(dlogits, out_weight, preferred_element_type=jnp.float32)  8.16 us
  transfers between devices with their start and end apart: 3, of which 2 were waited for; matrix products, arithmetic and copies ran while one was open for 2% of the time, Pallas kernels for 0%

profile of v1, /device:TPU:1, one launch (start us, length us, event | category | flops | bytes accessed | tf_op | source)
XLA Modules:
  0.0 389.6 jit_solution(1125466257712527983)
XLA Ops:
  7.2 0.9 broadcast_in_dim.6
  8.0 38.0 %all_to_all.15 = bf16[32,64,256]{2,1,0:T(8,128)(2,1)S(1)} all-to-all(bf16[32,64,256]{2,1,0:T(8,128)(2,1)S(1)} %broadcast_in_dim.6), channel_id=1, replica_groups=mesh['vocab_0'=8,'vocab_1'=4,'section_0'=4,'section_1'=2] {'vocab_0','vo..., dimensions={0} | all-to-all | bytes 2097152 | tf_op jit(solution)/shard_map/all_to_all | solution.py:14
  46.1 0.1 copy.9
  46.1 4.2 %stack.3 = bf16[8,64,8192]{2,1,0:T(8,128)(2,1)} broadcast(bf16[64,8192]{1,0:T(8,128)(2,1)S(1)} %bitcast.340), dimensions={1,2} | broadcast | bytes 9437184 | tf_op jit(solution)/shard_map/stack | solution.py:81
  50.4 0.0 copy-start
  50.4 0.0 slice-start
  50.4 7.8 %all-to-all-start.1 = ((bf16[8,64,8192]{2,1,0:T(8,128)(2,1)}), bf16[8,64,8192]{2,1,0:T(8,128)(2,1)}, u32[]{:S(2)}, u32[]{:S(2)}) async-start(bf16[8,64,8192]{2,1,0:T(8,128)(2,1)} %stack.3), calls=%async_computation.1 | async-start | bytes 16777216 | tf_op jit(solution)/shard_map/all_to_all | solution.py:81
  58.1 0.0 reduce-scatter.2.cloned.1.call-start
  58.1 0.0 copy-done
  58.1 93.7 %all-to-all-done.1 = bf16[8,64,8192]{2,1,0:T(8,128)(2,1)} async-done(((bf16[8,64,8192]{2,1,0:T(8,128)(2,1)}), bf16[8,64,8192]{2,1,0:T(8,128)(2,1)}, u32[]{:S(2)}, u32[]{:S(2)}) %all-to-all-start.1) | async-done | bytes 8388640 | tf_op jit(solution)/shard_map/all_to_all | solution.py:81
  151.9 0.0 slice-start.1
  151.9 8.7 %fusion.60 = (f32[512]{0:T(512)S(1)}, f32[512,384]{0,1:T(8,128)S(1)}) fusion(bf16[512,8192]{1,0:T(8,128)(2,1)} %bitcast.1, bf16[384,8192]{1,0:T(8,128)(2,1)} %param.5), kind=kOutput, calls=%fused_computation.116 | convolution fusion | flops 3221421568 | bytes 15468544 | tf_op jit(solution)/shard_map/td,vd->tv/dot_general | solution.py:86
  160.6 0.2 exponential_reduce_fusion
  160.9 18.9 %all-gather.4 = f32[8,3,512]{2,1,0:T(4,128)S(1)} all-gather(f32[1,3,512]{2,1,0:T(4,128)S(1)} %maximum_bitcast_fusion), channel_id=2, replica_groups=mesh['vocab_0'=8,'vocab_1'=4,'section_0'=4,'section_1'=2] {'vocab_0'}, dimensions={0}, use_global_device_ids=true | all-gather | bytes 55296 | tf_op jit(solution)/shard_map/all_gather | solution.py:36
  179.8 0.1 fusion.22
  179.9 9.7 %all-gather.5 = f32[4,3,512]{2,1,0:T(4,128)S(1)} all-gather(f32[1,3,512]{2,1,0:T(4,128)S(1)} %maximum_bitcast_fusion.1), channel_id=3, replica_groups=mesh['vocab_0'=8,'vocab_1'=4,'section_0'=4,'section_1'=2] {'vocab_1'}, dimensions={0}, use_global_device_ids=true | all-gather | bytes 30720 | tf_op jit(solution)/shard_map/all_gather | solution.py:36
  189.7 9.0 %all-gather.6 = f32[4,3,512]{2,1,0:T(4,128)S(1)} all-gather(f32[1,3,512]{2,1,0:T(4,128)S(1)} %maximum_bitcast_fusion.2), channel_id=4, replica_groups=mesh['vocab_0'=8,'vocab_1'=4,'section_0'=4,'section_1'=2] {'section_0'}, dimensions={0}, use_global_device_ids=true | all-gather | bytes 30720 | tf_op jit(solution)/shard_map/all_gather | solution.py:36
  198.8 13.8 %all-gather.7 = f32[2,3,512]{2,1,0:T(4,128)S(1)} all-gather(f32[1,3,512]{2,1,0:T(4,128)S(1)} %maximum_bitcast_fusion.3), channel_id=5, replica_groups=mesh['vocab_0'=8,'vocab_1'=4,'section_0'=4,'section_1'=2] {'section_1'}, dimensions={0}, use_global_device_ids=true | all-gather | bytes 18432 | tf_op jit(solution)/shard_map/all_gather | solution.py:36
  212.7 0.6 add_subtract_fusion
  213.3 0.0 slice-done
  213.3 0.0 slice-done.1
  213.3 8.2 %fusion.55 = f32[512,8192]{1,0:T(8,128)} fusion(bf16[384,8192]{1,0:T(8,128)(2,1)S(1)} %bitcast.339, f32[512,384]{0,1:T(8,128)S(1)} %get-tuple-element.20, f32[512]{0:T(512)S(1)} %get-tuple-element.6, f32[512]{0:T(512)S(1)} %get-tuple-element.7, s32[512]{0:T(512)S(1)} %broadcast_subtract_fusion), kind=kOutput, calls=%fused_computation.114 | convolution fusion | flops 3222405120 | bytes 23861248 | tf_op jit(solution)/shard_map/dot_general | solution.py:101
  221.4 0.0 reduce-scatter.2.cloned.1.call-update
  221.5 89.2 %reduce-scatter.2.cloned.1.call-done = f32[64,8192]{1,0:T(8,128)} async-done(((f32[512,8192]{1,0:T(8,128)}), f32[64,8192]{1,0:T(8,128)}) %reduce-scatter.2.cloned.1.call-update) | async-done | bytes 2097168 | tf_op jit(solution)/shard_map/reduce_scatter | solution.py:100
  310.6 1.8 copy.11
  312.4 57.7 %all_to_all.16 = f32[32,64,256]{2,1,0:T(8,128)S(1)} all-to-all(f32[32,64,256]{2,1,0:T(8,128)S(1)} %bitcast.337), channel_id=1, replica_groups=mesh['vocab_0'=8,'vocab_1'=4,'section_0'=4,'section_1'=2] {'vocab_0','vo..., dimensions={0} | all-to-all | bytes 4194304 | tf_op jit(solution)/shard_map/all_to_all | solution.py:61
  370.1 0.1 reduce_sum.29
  370.3 3.1 collective-permute-start
  373.4 8.7 %convolution_convert_fusion = bf16[384,8192]{1,0:T(8,128)(2,1)} fusion(bf16[512,8192]{1,0:T(8,128)(2,1)} %bitcast.1, f32[512,384]{0,1:T(8,128)S(1)} %get-tuple-element.20, f32[512]{0:T(512)S(1)} %get-tuple-element.6, f32[512]{0:T(512)S(1)} %get-tuple-element.7, s32[512]{0:T(512)S(1)} %broadcast_subtract_fusion), kind=kOutput, calls=%fused_computation | convolution fusion | flops 3225550848 | bytes 15472640 | tf_op jit(solution)/shard_map/tv,td->vd/dot_general | solution.py:97
  382.1 0.0 collective-permute-done
  382.1 0.6 copy.13
  (12 shorter events, 0.2 us)
Async XLA Ops:
  50.4 7.8 %copy-start = (s32[512]{0:T(512)S(1)}, s32[512]{0:T(512)}, u32[]{:S(2)}) copy-start(s32[512]{0:T(512)} %param.4) | copy-start | bytes 6148
  50.4 162.9 %slice-start = ((s8[6291456]{0:T(1024)(128)(4,1)}), s8[2097152]{0:T(1024)(128)(4,1)S(1)}, s32[]{:S(2)}) async-start(s8[6291456]{0:T(1024)(128)(4,1)} %bitcast.338), calls=%async_computation.5 | async-start | bytes 4194304
  50.4 101.5 %all-to-all-start.1 = ((bf16[8,64,8192]{2,1,0:T(8,128)(2,1)}), bf16[8,64,8192]{2,1,0:T(8,128)(2,1)}, u32[]{:S(2)}, u32[]{:S(2)}) async-start(bf16[8,64,8192]{2,1,0:T(8,128)(2,1)} %stack.3), calls=%async_computation.1 | async-start | bytes 16777216 | tf_op jit(solution)/shard_map/all_to_all | solution.py:81
  58.1 252.5 %reduce-scatter.2.cloned.1.call-start = ((), (), s32[]{:S(2)}) async-start(), calls=%async_computation.4 | async-start | bytes 18874368 | tf_op jit(solution)/shard_map/reduce_scatter | solution.py:100
  151.9 61.4 %slice-start.1 = ((s8[6291456]{0:T(1024)(128)(4,1)}), s8[4194304]{0:T(1024)(128)(4,1)S(1)}, s32[]{:S(2)}) async-start(s8[6291456]{0:T(1024)(128)(4,1)} %bitcast.338), calls=%async_computation.6 | async-start | bytes 8388608
  370.3 11.8 %collective-permute-start = (bf16[64,256]{1,0:T(8,128)(2,1)S(1)}, bf16[64,256]{1,0:T(8,128)(2,1)S(1)}, u32[]{:S(2)}, u32[]{:S(2)}) collective-permute-start(bf16[64,256]{1,0:T(8,128)(2,1)S(1)} %reduce_sum.29), channel_id=1, source_target_pairs={{0,7},{1,0},{2,1},{3,2},{4,3},{5,4},{6,5},{7,6},{8,15},{9,8},{10,9... | collective-permute-start | bytes 98312 | tf_op jit(solution)/shard_map/ppermute | solution.py:68
Sparse Core Ops, SparseCore 0:
  221.6 88.9 reduce-scatter.1
